TPU v7x, 128 devices: a whole 4x4x4 slice. The times are simulated.
128 devices in a mesh: lat: 32 (over z, y, x_hi), lev: 4 (over x_lo, core).
Axes of the slice: x: 4 (x_hi: 2, x_lo: 2; x = x_hi * 2 + x_lo), y: 4, z: 4, core: 2. Of those that a mesh axis runs over, the one named last changes fastest.
Arguments:
- spec_in: bfloat16 [192, 171, 4, 512], P('lat', None, None, 'lev'), may hold values from -6 to 6
- cotangent: bfloat16 [192, 171, 4, 512], P('lat', None, None, 'lev'), may hold values from -6 to 6
- legendre: bfloat16 [192, 171, 256], P('lat'), may hold values from -0.4375 to 0.4375
- quad_weights: float32 [256], replicated, may hold values from 0.5 to 2
- wave_order: int32 [192], replicated, may hold values from 0 to 191, each once
- norm_gain: float32 [256], replicated, may hold values from 0.5 to 1.5
- weight_in: bfloat16 [256, 512], replicated, may hold values from -0.375 to 0.375
- bias_in: float32 [512], replicated, may hold values from -3 to 3
- weight_mid: bfloat16 [512, 512], replicated, may hold values from -0.25 to 0.25
- bias_mid: float32 [512], replicated, may hold values from -3 to 3
- weight_out: bfloat16 [512, 256], replicated, may hold values from -0.25 to 0.25
Outputs:
- grad_spec: float32 [192, 171, 4, 512], P('lat', None, None, 'lev')
- grad_gain: float32 [256], replicated
- grad_w_in: float32 [256, 512], replicated
- grad_b_in: float32 [512], replicated
- grad_w_mid: float32 [512, 512], replicated
- grad_b_mid: float32 [512], replicated
- grad_w_out: float32 [512, 256], replicated
Inputs may be any that keep to these rules, and one draw needn't show every extreme that they name: `wave_order`: each of 0 to 191 appears once; a slot holding 171 or more is unused.
All inputs are finite; a program needn't handle non-finite values.
Results may differ from a plain program's by a relative error of at most 0.007.
Values may be sent and summed in bfloat16 or wider, within the bound.
A program may use at most 128 MiB of HBM per device.

v0:
```python
import math
import jax
import jax.numpy as jnp
from jax import lax
from jax.sharding import PartitionSpec as P

WAVES = 171
NLAT = 256
NLON = 512
MEMBERS = 4
time_step = 0.5
norm_eps = 1e-06


def in_one_piece(arrays, axis, split_dim, concat_dim, along):
    ends, at = ([], 0)
    for a in arrays[:-1]:
        at += a.shape[along]
        ends.append(at)
    both = jnp.concatenate(arrays, axis=along)
    return tuple(
        jnp.split(
            lax.all_to_all(both, axis, split_axis=split_dim, concat_axis=concat_dim, tiled=True),
            ends,
            axis=along,
        )
    )


def spectral_masks(waves_held, degree_count):
    degree = jnp.arange(degree_count, dtype=jnp.int32)
    living = (waves_held[:, None] <= degree[None, :]) & (waves_held[:, None] < WAVES)
    ratio = (degree * (degree + 1)).astype(jnp.float32) / float(WAVES * (WAVES - 1))
    factor = 1.0 / (1.0 + ratio * ratio)
    shrink = jnp.where(living, factor[None, :], jnp.zeros_like(factor)[None, :])
    return (living, shrink)


def fourier_table(waves_all):
    longitude = jnp.arange(NLON, dtype=jnp.int32)
    phase_steps = waves_all[:, None] * longitude[None, :] % NLON
    angles = phase_steps.astype(jnp.float32) * (2.0 * math.pi / NLON)
    weight_scale = jnp.where(waves_all < WAVES, math.sqrt(2.0 / NLON), 0.0).astype(jnp.float32)[
        :, None
    ]
    return jnp.stack(
        [jnp.cos(angles) * weight_scale, -jnp.sin(angles) * weight_scale], axis=1
    ).astype(jnp.bfloat16)


def contract_rows(left, right):
    return lax.dot_general(
        left, right, (((0,), (0,)), ((), ())), preferred_element_type=jnp.float32
    )


def contract_cols(left, right):
    return lax.dot_general(
        left, right, (((1,), (1,)), ((), ())), preferred_element_type=jnp.float32
    )


def column_grads(
    columns, column_cot, norm_gain, weight_in, bias_in, weight_mid, bias_mid, weight_out
):
    inputs = columns.astype(jnp.float32)
    inverse = lax.rsqrt(jnp.mean(inputs * inputs, axis=1, keepdims=True) + norm_eps)
    normed = (inputs * inverse * norm_gain).astype(jnp.bfloat16)
    pre_one = jnp.dot(normed, weight_in, preferred_element_type=jnp.float32) + bias_in
    sig_one = jax.nn.sigmoid(pre_one)
    act_one = (pre_one * sig_one).astype(jnp.bfloat16)
    pre_two = jnp.dot(act_one, weight_mid, preferred_element_type=jnp.float32) + bias_mid
    sig_two = jax.nn.sigmoid(pre_two)
    act_two = (pre_two * sig_two).astype(jnp.bfloat16)
    gradient_third = contract_rows(act_two, column_cot)
    back_two = contract_cols(column_cot, weight_out)
    delta_two = (back_two * sig_two * (1.0 + pre_two * (1.0 - sig_two))).astype(jnp.bfloat16)
    gradient_second = contract_rows(act_one, delta_two)
    offset_second = jnp.sum(delta_two.astype(jnp.float32), axis=0)
    back_one = contract_cols(delta_two, weight_mid)
    delta_one = (back_one * sig_one * (1.0 + pre_one * (1.0 - sig_one))).astype(jnp.bfloat16)
    gradient_first = contract_rows(normed, delta_one)
    offset_first = jnp.sum(delta_one.astype(jnp.float32), axis=0)
    back_norm = contract_cols(delta_one, weight_in)
    gradient_gain = jnp.sum(back_norm * inputs * inverse, axis=0)
    scaled = back_norm * norm_gain
    grad_columns = inverse * scaled - inputs * inverse * inverse * inverse * jnp.mean(
        scaled * inputs, axis=1, keepdims=True
    )
    return (
        grad_columns.astype(jnp.bfloat16),
        (
            gradient_gain,
            gradient_first,
            offset_first,
            gradient_second,
            offset_second,
            gradient_third,
        ),
    )


def synthesize(wave_table, coeffs):
    shape = coeffs.shape
    split = coeffs.reshape(shape[0], shape[1], shape[2], shape[3] // 2, 2)
    return jnp.einsum(
        "spo,stecp->otec", wave_table, split, preferred_element_type=jnp.float32
    ).astype(jnp.bfloat16)


def analyze(wave_table, values):
    result = jnp.einsum(
        "spo,otec->stecp", wave_table, values, preferred_element_type=jnp.float32
    ).astype(jnp.bfloat16)
    shape = result.shape
    return result.reshape(shape[0], shape[1], shape[2], shape[3] * 2)


def local(
    spec_in,
    cotangent,
    legendre,
    quad_weights,
    wave_order,
    norm_gain,
    weight_in,
    bias_in,
    weight_mid,
    bias_mid,
    weight_out,
):
    slots_here = spec_in.shape[0]
    own_waves = lax.dynamic_slice_in_dim(wave_order, lax.axis_index("lat") * slots_here, slots_here)
    living, shrink = spectral_masks(own_waves, spec_in.shape[1])
    basis_rows = jnp.where(living[:, :, None], legendre, jnp.zeros_like(legendre))
    wave_table = fourier_table(wave_order)
    fourier = jnp.einsum(
        "slt,slek->stek", basis_rows, spec_in, preferred_element_type=jnp.float32
    ).astype(jnp.bfloat16)
    pushed = (time_step * cotangent.astype(jnp.float32) * shrink[:, :, None, None]).astype(
        jnp.bfloat16
    )
    pulled = jnp.einsum("slt,slek->stek", basis_rows, pushed, preferred_element_type=jnp.float32)
    pulled = (quad_weights[None, :, None, None] * pulled).astype(jnp.bfloat16)
    fourier_all, pulled_all = in_one_piece((fourier, pulled), "lat", 1, 0, 2)
    grid_part = synthesize(wave_table, fourier_all)
    cot_part = synthesize(wave_table, pulled_all)
    grid_values, grid_cot = in_one_piece((grid_part, cot_part), "lev", 0, 3, 1)
    grid_shape = grid_values.shape
    grad_rows, grads_local = column_grads(
        grid_values.reshape(-1, grid_shape[3]),
        grid_cot.reshape(-1, grid_shape[3]),
        norm_gain,
        weight_in,
        bias_in,
        weight_mid,
        bias_mid,
        weight_out,
    )
    grad_grid = grad_rows.reshape(grid_shape)
    grad_part = lax.all_to_all(grad_grid, "lev", split_axis=3, concat_axis=0, tiled=True)
    back_fourier = analyze(wave_table, grad_part)
    back_slots = lax.all_to_all(back_fourier, "lat", split_axis=0, concat_axis=1, tiled=True)
    summed = lax.psum(
        (
            grads_local[0],
            grads_local[1],
            grads_local[2],
            grads_local[3],
            grads_local[4],
            grads_local[5],
        ),
        ("lat", "lev"),
    )
    factor = float(MEMBERS * NLAT * NLON) ** (-0.5)
    grads = tuple((piece * factor for piece in summed))
    grad_spec = cotangent.astype(jnp.float32) * shrink[:, :, None, None] + jnp.einsum(
        "slt,stek->slek", basis_rows, back_slots, preferred_element_type=jnp.float32
    )
    return (grad_spec, grads[0], grads[1], grads[2], grads[3], grads[4], grads[5])


def solution(mesh):
    placed = (
        P("lat", None, None, "lev"),
        P("lat", None, None, "lev"),
        P("lat", None, None),
        P(),
        P(),
        P(),
        P(),
        P(),
        P(),
        P(),
        P(),
    )
    return jax.shard_map(
        local,
        mesh=mesh,
        in_specs=placed,
        out_specs=(P("lat", None, None, "lev"), P(), P(), P(), P(), P(), P()),
        check_vma=False,
    )
```

profile of v0, /device:TPU:1, one launch (start us, length us, event | category | flops | bytes accessed | tf_op | source)
XLA Modules:
  0.0 443.2 jit_solution(5164331908292639618)
XLA Ops:
  7.2 0.0 copy-start
  7.2 0.8 broadcast_compare_fusion
  8.0 0.1 fusion.29
  8.1 0.7 broadcast_select_fusion.4
  8.8 1.9 convolution_convert_fusion
  10.7 2.4 multiply_convert_fusion.6
  13.2 0.3 pad_maximum_fusion.1
  13.5 3.7 copy.95
  17.2 12.1 %all-to-all-start = ((bf16[6,256,8,128]{3,2,0,1:T(8,128)(2,1)}), bf16[6,256,8,128]{3,2,0,1:T(8,128)(2,1)}, u32[]{:S(2)}, u32[]{:S(2)}) async-start(bf16[6,256,8,128]{3,2,0,1:T(8,128)(2,1)} %copy.95), calls=%async_computation | async-start | bytes 6291456 | tf_op jit(solution)/shard_map/all_to_all | solution.py:23
  29.3 1.9 multiply_convert_fusion.8
  31.2 38.7 %all-to-all-done = bf16[6,256,8,128]{3,2,0,1:T(8,128)(2,1)} async-done(((bf16[6,256,8,128]{3,2,0,1:T(8,128)(2,1)}), bf16[6,256,8,128]{3,2,0,1:T(8,128)(2,1)}, u32[]{:S(2)}, u32[]{:S(2)}) %all-to-all-start) | async-done | bytes 3145760 | tf_op jit(solution)/shard_map/all_to_all | solution.py:23
  69.9 2.7 copy.97
  72.7 2.2 fusion.45
  74.9 5.3 %copy.98 = bf16[192,8,4,128]{0,1,3,2:T(8,128)(2,1)} copy(bf16[192,8,4,128]{3,2,1,0:T(4,128)(2,1)} %get-tuple-element.61) | data formatting | bytes 3145728 | tf_op jit(solution)/shard_map/split | solution.py:22
  80.2 4.2 copy.100
  84.4 3.7 bitcast_convert_fusion.1
  88.2 2.1 bitcast_convert_fusion
  90.2 2.3 pad_maximum_fusion
  92.6 13.8 %copy.102 = bf16[512,16,4,64]{3,2,1,0:T(4,128)(2,1)} copy(bf16[512,16,4,64]{0,3,2,1:T(8,128)(2,1)} %pad_maximum_fusion) | data formatting | bytes 8388608 | tf_op jit(solution)/shard_map/concatenate | solution.py:20
  106.4 9.5 %reshape.301 = bf16[4,2,262144]{2,1,0:T(2,128)(2,1)} reshape(bf16[512,16,4,64]{3,2,1,0:T(4,128)(2,1)} %copy.102) | data formatting | bytes 8388608
  115.9 55.2 %all_to_all.72 = bf16[4,2,262144]{2,1,0:T(2,128)(2,1)} all-to-all(bf16[4,2,262144]{2,1,0:T(2,128)(2,1)} %reshape.301), channel_id=1, replica_groups=mesh['lat'=32,'lev'=4] {'lev'}, dimensions={0} | all-to-all | bytes 8388608 | tf_op jit(solution)/shard_map/all_to_all | solution.py:23
  171.1 9.3 %reshape.302 = bf16[512,16,4,64]{3,2,1,0:T(4,128)(2,1)} reshape(bf16[4,2,262144]{2,1,0:T(2,128)(2,1)} %all_to_all.72) | data formatting | bytes 8388608
  180.4 12.7 %copy.104 = bf16[128,16,4,4,64]{0,4,3,2,1:T(8,128)(2,1)} copy(bf16[128,16,4,4,64]{4,2,1,0,3:T(4,128)(2,1)} %bitcast.65) | data formatting | bytes 8388608 | tf_op jit(solution)/shard_map/all_to_all | solution.py:23
  193.1 2.0 multiply_reduce_fusion.2
  195.1 4.7 %fusion.44 = (bf16[128,8,4,256]{0,3,2,1:T(8,128)(2,1)S(1)}, f32[128,8,4,256]{0,3,2,1:T(8,128)}) fusion(bf16[128,16,4,256]{0,3,2,1:T(8,128)(2,1)} %bitcast.67), kind=kLoop, calls=%fused_computation.85 | loop fusion | flops 1048576 | bytes 10485760 | tf_op jit(solution)/shard_map/split | solution.py:22
  199.8 0.3 copy.106
  200.1 0.3 rsqrt.12
  200.4 2.9 copy.107
  203.2 2.5 reshape.291
  205.8 6.3 %copy.108 = f32[128,8,4,256]{3,2,1,0:T(4,128)} copy(f32[128,8,4,256]{0,3,2,1:T(8,128)} %get-tuple-element.60) | data formatting | bytes 8388608 | tf_op jit(solution)/shard_map/convert_element_type | solution.py:66
  212.1 5.4 %reshape.294 = f32[4096,256]{1,0:T(8,128)} reshape(f32[128,8,4,256]{3,2,1,0:T(4,128)} %copy.108) | data formatting | bytes 8388608 | tf_op jit(solution)/shard_map/convert_element_type | solution.py:66
  217.5 0.0 copy-start.9
  217.5 4.9 %multiply_convert_fusion.3 = (bf16[4096,512]{1,0:T(8,128)(2,1)S(1)}, f32[4096,512]{1,0:T(8,128)S(1)}) fusion(f32[512]{0:T(512)S(1)} %copy-done.17, bf16[256,512]{1,0:T(8,128)(2,1)S(1)} %copy-done.10, f32[4096,256]{1,0:T(8,128)} %reshape.294, f32[256]{0:T(256)S(1)} %copy-done.14, f32[4096]{0:T(1024)S(1)} %rsqrt.12), kind=kOutput, calls=%fused_computation.6 | convolution fusion | flops 1089470464 | bytes 17058816 | tf_op jit(solution)/shard_map/dot_general | solution.py:69
  222.4 0.0 copy-start.16
  222.4 2.4 fusion.46
  224.9 3.9 convert_reduce_fusion
  228.8 3.3 fusion.47
  232.1 4.4 %convert_reduce_fusion.1 = (f32[512]{0:T(512)S(1)}, bf16[4096,512]{1,0:T(8,128)(2,1)S(1)}) fusion(f32[4096,512]{1,0:T(8,128)S(1)} %get-tuple-element.68, f32[512]{0:T(512)S(1)} %copy-done.17, bf16[4096,512]{1,0:T(8,128)(2,1)S(1)} %get-tuple-element.73, bf16[512,512]{1,0:T(8,128)(2,1)S(1)} %copy-done.9), kind=kOutput, calls=%fused_computation.2 | convolution fusion | flops 2172648960 | bytes 17305600 | tf_op jit(solution)/shard_map/dot_general | solution.py:58
  236.6 1.9 multiply_reduce_fusion
  238.5 0.1 copy-done.3
  238.5 3.2 subtract_convert_fusion
  241.7 2.5 reshape.292
  244.3 4.1 copy.109
  248.4 4.7 %all-to-all-start.2 = ((bf16[128,8,4,256]{0,2,1,3:T(4,128)(2,1)}), bf16[128,8,4,256]{0,2,1,3:T(4,128)(2,1)S(1)}, u32[]{:S(2)}, u32[]{:S(2)}) async-start(bf16[128,8,4,256]{0,2,1,3:T(4,128)(2,1)} %copy.109), calls=%async_computation.2 | async-start | bytes 4194304 | tf_op jit(solution)/shard_map/all_to_all | solution.py:161
  253.0 6.9 %fusion.42 = f32[256,512]{1,0:T(8,128)} fusion(bf16[4096,512]{1,0:T(8,128)(2,1)} %copy-done.3, f32[4096,256]{1,0:T(8,128)} %reshape.294, f32[256]{0:T(256)S(1)} %copy-done.14, f32[4096]{0:T(1024)S(1)} %rsqrt.12), kind=kOutput, calls=%fused_computation.83 | convolution fusion | flops 1076887552 | bytes 8930304 | tf_op jit(solution)/shard_map/dot_general | solution.py:52
  259.9 6.6 %fusion = f32[512,256]{1,0:T(8,128)} fusion(bf16[4096,256]{1,0:T(8,128)(2,1)S(1)} %copy-done.8, f32[4096,512]{1,0:T(8,128)} %copy-done.4, f32[512]{0:T(512)S(1)} %copy-done.18), kind=kOutput, calls=%fused_computation.16 | convolution fusion | flops 1086324736 | bytes 11012096 | tf_op jit(solution)/shard_map/dot_general | solution.py:52
  266.6 0.0 all-reduce.4.cloned.1.call-update
  266.6 11.5 %all-to-all-done.2 = bf16[128,8,4,256]{0,2,1,3:T(4,128)(2,1)S(1)} async-done(((bf16[128,8,4,256]{0,2,1,3:T(4,128)(2,1)}), bf16[128,8,4,256]{0,2,1,3:T(4,128)(2,1)S(1)}, u32[]{:S(2)}, u32[]{:S(2)}) %all-to-all-start.2) | async-done | bytes 2097184 | tf_op jit(solution)/shard_map/all_to_all | solution.py:161
  278.1 0.8 copy.110
  278.9 2.0 copy.111
  280.8 2.5 reshape.299
  283.3 2.9 convert_bitcast_fusion
  286.2 1.2 copy.112
  287.4 3.2 copy.113
  290.6 8.0 %all-to-all-start.3 = ((bf16[192,8,4,128]{3,1,2,0:T(8,128)(2,1)}), bf16[192,8,4,128]{3,1,2,0:T(8,128)(2,1)S(1)}, u32[]{:S(2)}, u32[]{:S(2)}) async-start(bf16[192,8,4,128]{3,1,2,0:T(8,128)(2,1)} %copy.113), calls=%async_computation.3 | async-start | bytes 3145728 | tf_op jit(solution)/shard_map/all_to_all | solution.py:163
  298.6 76.6 %all-reduce = (f32[256]{0:T(256)S(1)}, f32[512]{0:T(512)S(1)}, f32[512]{0:T(512)S(1)}) all-reduce(f32[256]{0:T(256)S(1)} %get-tuple-element.49, f32[512]{0:T(512)S(1)} %get-tuple-element.70, f32[512]{0:T(512)S(1)} %get-tuple-element.72), channel_id=1, replica_groups=mesh['lat'=32,'lev'=4] {'lat','lev'}, use_global_device_ids=true, to_apply=%region_3.4 | all-reduce | flops 1280 | bytes 10240 | tf_op jit(solution)/shard_map/psum | solution.py:164
  375.3 0.6 broadcast_multiply_fusion.7
  375.8 0.6 broadcast_multiply_fusion.5
  376.4 49.5 %all-reduce.4.cloned.1.call-done = (f32[256,512]{1,0:T(8,128)}, f32[512,512]{1,0:T(8,128)}, f32[512,256]{1,0:T(8,128)}) async-done(((f32[256,512]{1,0:T(8,128)}, f32[512,512]{1,0:T(8,128)}, f32[512,256]{1,0:T(8,128)}), (f32[256,512]{1,0:T(8,128)}, f32[512,512]{1,0:T(8,128)}, f32[512,256]{1,0:T(8,128)})) %all-reduce.4.cloned.1.call-update) | async-done | bytes 2097168 | tf_op jit(solution)/shard_map/psum | solution.py:164
  425.9 1.9 broadcast_multiply_fusion.2
  427.8 1.9 broadcast_multiply_fusion.1
  429.7 2.3 broadcast_multiply_fusion
  432.0 1.9 fusion.1
  433.9 2.1 copy.115
  (40 shorter events, 0.1 us)
Async XLA Ops:
  7.2 1.6 copy-start
  8.1 2.6 copy-start.12
  17.2 12.1 %copy-start.15 = (s32[192]{0:T(256)S(1)}, s32[192]{0:T(256)}, u32[]{:S(2)}) copy-start(s32[192]{0:T(256)} %param.15) | copy-start | bytes 2308
  17.2 52.7 %all-to-all-start = ((bf16[6,256,8,128]{3,2,0,1:T(8,128)(2,1)}), bf16[6,256,8,128]{3,2,0,1:T(8,128)(2,1)}, u32[]{:S(2)}, u32[]{:S(2)}) async-start(bf16[6,256,8,128]{3,2,0,1:T(8,128)(2,1)} %copy.95), calls=%async_computation | async-start | bytes 6291456 | tf_op jit(solution)/shard_map/all_to_all | solution.py:23
  84.4 3.7 copy-start.6
  205.8 19.1 %copy-start.7 = (bf16[4096,256]{1,0:T(8,128)(2,1)}, bf16[4096,256]{1,0:T(8,128)(2,1)S(1)}, u32[]{:S(2)}) copy-start(bf16[4096,256]{1,0:T(8,128)(2,1)S(1)} %reshape.291) | copy-start | bytes 6291460
  212.1 5.4 %copy-start.10 = (bf16[256,512]{1,0:T(8,128)(2,1)S(1)}, bf16[256,512]{1,0:T(8,128)(2,1)}, u32[]{:S(2)}) copy-start(bf16[256,512]{1,0:T(8,128)(2,1)} %param.17) | copy-start | bytes 786436
  212.1 5.4 %copy-start.14 = (f32[256]{0:T(256)S(1)}, f32[256]{0:T(256)}, u32[]{:S(2)}) copy-start(f32[256]{0:T(256)} %param.16) | copy-start | bytes 3076
  212.1 5.4 %copy-start.17 = (f32[512]{0:T(512)S(1)}, f32[512]{0:T(512)}, u32[]{:S(2)}) copy-start(f32[512]{0:T(512)} %param.18) | copy-start | bytes 6148
  217.5 4.9 %copy-start.9 = (bf16[512,512]{1,0:T(8,128)(2,1)S(1)}, bf16[512,512]{1,0:T(8,128)(2,1)}, u32[]{:S(2)}) copy-start(bf16[512,512]{1,0:T(8,128)(2,1)} %param.19) | copy-start | bytes 1572868
  222.4 2.5 copy-start.16
  222.4 2.5 copy-start.18
  224.9 3.9 copy-start.4
  232.1 4.5 %copy-start.2 = (f32[4096,256]{1,0:T(8,128)S(1)}, f32[4096,256]{1,0:T(8,128)}, u32[]{:S(2)}) copy-start(f32[4096,256]{1,0:T(8,128)} %reshape.294) | copy-start | bytes 12582916
  236.6 1.9 copy-start.3
  248.4 29.7 %all-to-all-start.2 = ((bf16[128,8,4,256]{0,2,1,3:T(4,128)(2,1)}), bf16[128,8,4,256]{0,2,1,3:T(4,128)(2,1)S(1)}, u32[]{:S(2)}, u32[]{:S(2)}) async-start(bf16[128,8,4,256]{0,2,1,3:T(4,128)(2,1)} %copy.109), calls=%async_computation.2 | async-start | bytes 4194304 | tf_op jit(solution)/shard_map/all_to_all | solution.py:161
  253.0 172.9 %all-reduce.4.cloned.1.call-start = ((), (), s32[]{:S(2)}) async-start(), calls=%async_computation.4 | async-start | bytes 4194304 | tf_op jit(solution)/shard_map/psum | solution.py:164
  253.0 6.9 %copy-start.8 = (bf16[4096,256]{1,0:T(8,128)(2,1)S(1)}, bf16[4096,256]{1,0:T(8,128)(2,1)}, u32[]{:S(2)}) copy-start(bf16[4096,256]{1,0:T(8,128)(2,1)} %copy-done.7) | copy-start | bytes 6291460
  290.6 141.4 %copy-start.5 = (bf16[6,171,256]{2,1,0:T(8,128)(2,1)S(1)}, bf16[6,171,256]{2,1,0:T(8,128)(2,1)}, u32[]{:S(2)}) copy-start(bf16[6,171,256]{2,1,0:T(8,128)(2,1)} %param.13) | copy-start | bytes 1575940
  290.6 141.4 %copy-start.11 = (f32[6,171]{1,0:T(8,128)S(1)}, f32[6,171]{1,0:T(8,128)}, u32[]{:S(2)}) copy-start(f32[6,171]{1,0:T(8,128)} %get-tuple-element.63) | copy-start | bytes 12316
  290.6 141.4 %copy-start.13 = (pred[6,171]{1,0:T(8,128)(4,1)S(1)}, pred[6,171]{1,0:T(8,128)(4,1)}, u32[]{:S(2)}) copy-start(pred[6,171]{1,0:T(8,128)(4,1)} %copy-done.12) | copy-start | bytes 3082
  290.6 141.4 %all-to-all-start.3 = ((bf16[192,8,4,128]{3,1,2,0:T(8,128)(2,1)}), bf16[192,8,4,128]{3,1,2,0:T(8,128)(2,1)S(1)}, u32[]{:S(2)}, u32[]{:S(2)}) async-start(bf16[192,8,4,128]{3,1,2,0:T(8,128)(2,1)} %copy.113), calls=%async_computation.3 | async-start | bytes 3145728 | tf_op jit(solution)/shard_map/all_to_all | solution.py:163
  432.0 4.1 copy-start.1
Sparse Core Ops, SparseCore 0:
  266.7 159.1 all-reduce.3
where the time goes:
time: 449 us; the launch traced here: 443 us
  blocking collectives  132 us (29%)
  local copies, waits for them, and re-layouts  99.7 us (22%)
  waiting for transfers between devices  99.7 us (22%)
  matrix products  49.4 us (11%)
  starting transfers between devices  24.8 us (6%)
  other arithmetic  23.3 us (5%)
  between operations  14.6 us (3%)
    psum x1, blocking collectives, local(): lax.psum((grads_local[0], grads_local[1], grads_local[2], grads_local[3],...  76.6 us
    all_to_all x1, blocking collectives, in_one_piece(): lax.all_to_all(both, axis, split_axis=split_dim, concat_axis=concat_dim,...  55.2 us
    psum x1, waiting for transfers between devices, local(): lax.psum((grads_local[0], grads_local[1], grads_local[2], grads_local[3],...  49.5 us
    all_to_all x1, waiting for transfers between devices, in_one_piece(): lax.all_to_all(both, axis, split_axis=split_dim, concat_axis=concat_dim,...  38.7 us
    unnamed x41, local copies, waits for them, and re-layouts  21.1 us
    concatenate x2, local copies, waits for them, and re-layouts, in_one_piece(): both = jnp.concatenate(arrays, axis=along)  17.5 us
    dot_general x3, matrix products, contract_rows(): lax.dot_general(left, right, (((0,), (0,)), ((), ())), preferred_element_...  16.9 us
    all_to_all x2, local copies, waits for them, and re-layouts, in_one_piece(): lax.all_to_all(both, axis, split_axis=split_dim, concat_axis=concat_dim,...  15.5 us
  transfers between devices with their start and end apart: 4, of which 3 were waited for; matrix products, arithmetic and copies ran while one was open for 8% of the time, Pallas kernels for 0%

commit v1 on v0

--- a/solution.py
+++ b/solution.py
@@ -162,15 +162,18 @@
     back_fourier = analyze(wave_table, grad_part)
     back_slots = lax.all_to_all(back_fourier, "lat", split_axis=0, concat_axis=1, tiled=True)
     summed = lax.psum(
-        (
-            grads_local[0],
-            grads_local[1],
-            grads_local[2],
-            grads_local[3],
-            grads_local[4],
-            grads_local[5],
+        lax.psum(
+            (
+                grads_local[0],
+                grads_local[1],
+                grads_local[2],
+                grads_local[3],
+                grads_local[4],
+                grads_local[5],
+            ),
+            "lat",
         ),
-        ("lat", "lev"),
+        "lev",
     )
     factor = float(MEMBERS * NLAT * NLON) ** (-0.5)
     grads = tuple((piece * factor for piece in summed))

time: 449 us -> 774 us (1.72)
  waiting for transfers between devices: 99.7 us -> 325 us
  blocking collectives: 132 us -> 235 us
    psum x1, waiting for transfers between devices: 49.5 us -> 287 us  [local(): lax.psum((grads_local[0], grads_local[1], grads_local[2], grads_local[3],...]
    psum x0 -> x1, blocking collectives: none -> 52.4 us  [local(): lax.psum(lax.psum((grads_local[0], grads_local[1], grads_local[2], grads_...]
    all_to_all x0 -> x1, blocking collectives: none -> 38.5 us  [local(): lax.all_to_all(grad_grid, 'lev', split_axis=3, concat_axis=0, tiled=True)]
    psum x1, blocking collectives: 76.6 us -> 88.9 us  [local(): lax.psum((grads_local[0], grads_local[1], grads_local[2], grads_local[3],...]
    all_to_all x1 -> x0, waiting for transfers between devices: 11.5 us -> none  [local(): lax.all_to_all(grad_grid, 'lev', split_axis=3, concat_axis=0, tiled=True)]
    unnamed x41 -> x33, local copies, waits for them, and re-layouts: 21.1 us -> 23 us
  transfers between devices with their start and end apart: 4 -> 4, of which waited for: 3 -> 2; matrix products, arithmetic and copies ran while one was open for 8% -> 4% of each run, Pallas kernels for 0% -> 0%
where the time goes in v1:
time: 774 us; the launch traced here: 768 us
  waiting for transfers between devices  325 us (42%)
  blocking collectives  235 us (30%)
  local copies, waits for them, and re-layouts  100 us (13%)
  matrix products  47.7 us (6%)
  other arithmetic  25.1 us (3%)
  starting transfers between devices  20.4 us (3%)
  between operations  14.6 us (2%)
    psum x1, waiting for transfers between devices, local(): lax.psum((grads_local[0], grads_local[1], grads_local[2], grads_local[3],...  287 us
    psum x1, blocking collectives, local(): lax.psum((grads_local[0], grads_local[1], grads_local[2], grads_local[3],...  88.9 us
    all_to_all x1, blocking collectives, in_one_piece(): lax.all_to_all(both, axis, split_axis=split_dim, concat_axis=concat_dim,...  55.2 us
    psum x1, blocking collectives, local(): lax.psum(lax.psum((grads_local[0], grads_local[1], grads_local[2], grads_...  52.4 us
    all_to_all x1, blocking collectives, local(): lax.all_to_all(grad_grid, 'lev', split_axis=3, concat_axis=0, tiled=True)  38.5 us
    all_to_all x1, waiting for transfers between devices, in_one_piece(): lax.all_to_all(both, axis, split_axis=split_dim, concat_axis=concat_dim,...  38.2 us
    unnamed x33, local copies, waits for them, and re-layouts  23 us
    concatenate x2, local copies, waits for them, and re-layouts, in_one_piece(): both = jnp.concatenate(arrays, axis=along)  17.5 us
  transfers between devices with their start and end apart: 4, of which 2 were waited for; matrix products, arithmetic and copies ran while one was open for 4% of the time, Pallas kernels for 0%

profile of v1, /device:TPU:1, one launch (start us, length us, event | category | flops | bytes accessed | tf_op | source)
XLA Modules:
  0.0 768.2 jit_solution(4520741918143475056)
XLA Ops:
  7.2 0.8 broadcast_compare_fusion
  8.0 0.1 fusion.29
  8.1 0.7 broadcast_select_fusion.4
  8.8 1.9 convolution_convert_fusion
  10.7 2.4 multiply_convert_fusion.6
  13.2 0.3 pad_maximum_fusion.1
  13.5 3.7 copy.95
  17.1 11.6 %all-to-all-start = ((bf16[6,256,8,128]{3,2,0,1:T(8,128)(2,1)}), bf16[6,256,8,128]{3,2,0,1:T(8,128)(2,1)}, u32[]{:S(2)}, u32[]{:S(2)}) async-start(bf16[6,256,8,128]{3,2,0,1:T(8,128)(2,1)} %copy.95), calls=%async_computation | async-start | bytes 6291456 | tf_op jit(solution)/shard_map/all_to_all | solution.py:23
  28.7 0.5 all-reduce.7.cloned.1.call-start
  29.3 1.9 multiply_convert_fusion.8
  31.2 38.2 %all-to-all-done = bf16[6,256,8,128]{3,2,0,1:T(8,128)(2,1)} async-done(((bf16[6,256,8,128]{3,2,0,1:T(8,128)(2,1)}), bf16[6,256,8,128]{3,2,0,1:T(8,128)(2,1)}, u32[]{:S(2)}, u32[]{:S(2)}) %all-to-all-start) | async-done | bytes 3145760 | tf_op jit(solution)/shard_map/all_to_all | solution.py:23
  69.4 2.7 copy.97
  72.1 2.2 fusion.45
  74.3 5.3 copy.98
  79.7 4.2 copy.100
  83.9 3.7 bitcast_convert_fusion.1
  87.7 2.1 bitcast_convert_fusion
  89.7 2.3 pad_maximum_fusion
  92.0 13.8 %copy.102 = bf16[512,16,4,64]{3,2,1,0:T(4,128)(2,1)} copy(bf16[512,16,4,64]{0,3,2,1:T(8,128)(2,1)} %pad_maximum_fusion) | data formatting | bytes 8388608 | tf_op jit(solution)/shard_map/concatenate | solution.py:20
  105.8 9.5 %reshape.301 = bf16[4,2,262144]{2,1,0:T(2,128)(2,1)} reshape(bf16[512,16,4,64]{3,2,1,0:T(4,128)(2,1)} %copy.102) | data formatting | bytes 8388608
  115.3 55.2 %all_to_all.72 = bf16[4,2,262144]{2,1,0:T(2,128)(2,1)} all-to-all(bf16[4,2,262144]{2,1,0:T(2,128)(2,1)} %reshape.301), channel_id=1, replica_groups=mesh['lat'=32,'lev'=4] {'lev'}, dimensions={0} | all-to-all | bytes 8388608 | tf_op jit(solution)/shard_map/all_to_all | solution.py:23
  170.5 9.3 %reshape.302 = bf16[512,16,4,64]{3,2,1,0:T(4,128)(2,1)} reshape(bf16[4,2,262144]{2,1,0:T(2,128)(2,1)} %all_to_all.72) | data formatting | bytes 8388608
  179.8 12.7 %copy.104 = bf16[128,16,4,4,64]{0,4,3,2,1:T(8,128)(2,1)} copy(bf16[128,16,4,4,64]{4,2,1,0,3:T(4,128)(2,1)} %bitcast.65) | data formatting | bytes 8388608 | tf_op jit(solution)/shard_map/all_to_all | solution.py:23
  192.5 2.0 multiply_reduce_fusion.2
  194.5 4.7 fusion.44
  199.3 0.3 copy.106
  199.5 0.3 rsqrt.12
  199.8 2.9 copy.107
  202.7 2.5 reshape.291
  205.2 5.5 copy.108
  210.7 5.3 reshape.294
  216.1 4.9 multiply_convert_fusion.3
  221.1 2.4 fusion.46
  223.5 3.4 fusion
  226.9 3.8 convert_reduce_fusion
  230.7 3.3 fusion.47
  234.1 4.5 convert_reduce_fusion.1
  238.6 2.0 copy-done.3
  240.5 3.3 fusion.42
  243.9 6.9 multiply_reduce_fusion
  250.8 0.0 all-reduce.7.cloned.1.call-update
  250.8 0.0 all-reduce.9.cloned.1.call-start
  250.8 5.1 subtract_convert_fusion
  255.9 2.5 reshape.292
  258.5 4.1 copy.109
  262.5 38.5 %all_to_all.73 = bf16[128,8,4,256]{0,2,1,3:T(4,128)(2,1)S(1)} all-to-all(bf16[128,8,4,256]{0,2,1,3:T(4,128)(2,1)} %copy.109), channel_id=1, replica_groups=mesh['lat'=32,'lev'=4] {'lev'}, dimensions={3} | all-to-all | bytes 4194304 | tf_op jit(solution)/shard_map/all_to_all | solution.py:161
  301.0 0.8 copy.110
  301.8 2.0 copy.111
  303.8 2.2 reshape.299
  306.0 286.8 %all-reduce.7.cloned.1.call-done = (f32[256,512]{1,0:T(8,128)}, f32[512,512]{1,0:T(8,128)}, f32[512,256]{1,0:T(8,128)}) async-done(((f32[256,512]{1,0:T(8,128)}, f32[512,512]{1,0:T(8,128)}, f32[512,256]{1,0:T(8,128)}), (f32[256,512]{1,0:T(8,128)}, f32[512,512]{1,0:T(8,128)}, f32[512,256]{1,0:T(8,128)})) %all-reduce.7.cloned.1.call-update) | async-done | bytes 2097168 | tf_op jit(solution)/shard_map/psum | solution.py:165
  592.8 0.0 all-reduce.9.cloned.1.call-update
  592.8 2.9 convert_bitcast_fusion
  595.7 1.2 copy.112
  596.9 3.2 copy.113
  600.1 8.3 %all-to-all-start.3 = ((bf16[192,8,4,128]{3,1,2,0:T(8,128)(2,1)}), bf16[192,8,4,128]{3,1,2,0:T(8,128)(2,1)S(1)}, u32[]{:S(2)}, u32[]{:S(2)}) async-start(bf16[192,8,4,128]{3,1,2,0:T(8,128)(2,1)} %copy.113), calls=%async_computation.3 | async-start | bytes 3145728 | tf_op jit(solution)/shard_map/all_to_all | solution.py:163
  608.4 88.9 %all-reduce = (f32[256]{0:T(256)S(1)}, f32[512]{0:T(512)S(1)}, f32[512]{0:T(512)S(1)}) all-reduce(f32[256]{0:T(256)S(1)} %get-tuple-element.49, f32[512]{0:T(512)S(1)} %get-tuple-element.76, f32[512]{0:T(512)S(1)} %get-tuple-element.78), channel_id=1, replica_groups=mesh['lat'=32,'lev'=4] {'lat'}, use_global_device_ids=true, to_apply=%region_3.4 | all-reduce | flops 1280 | bytes 10240 | tf_op jit(solution)/shard_map/psum | solution.py:165
  697.3 52.4 %all-reduce.2 = (f32[256]{0:T(256)S(1)}, f32[512]{0:T(512)S(1)}, f32[512]{0:T(512)S(1)}) all-reduce(f32[256]{0:T(256)S(1)} %get-tuple-element.51, f32[512]{0:T(512)S(1)} %get-tuple-element.52, f32[512]{0:T(512)S(1)} %get-tuple-element.53), channel_id=1, replica_groups=mesh['lat'=32,'lev'=4] {'lev'}, use_global_device_ids=true, to_apply=%region_4.5 | all-reduce | flops 1280 | bytes 10240 | tf_op jit(solution)/shard_map/psum | solution.py:164
  749.7 0.6 broadcast_multiply_fusion.7
  750.2 0.6 broadcast_multiply_fusion.5
  750.9 2.0 fusion.1
  752.9 2.1 copy.115
  755.0 1.9 broadcast_multiply_fusion.2
  756.9 1.9 broadcast_multiply_fusion.1
  758.8 2.3 broadcast_multiply_fusion
  (35 shorter events, 0.1 us)
Async XLA Ops:
  7.2 1.6 copy-start
  8.1 2.6 copy-start.8
  17.1 12.1 %copy-start.11 = (s32[192]{0:T(256)S(1)}, s32[192]{0:T(256)}, u32[]{:S(2)}) copy-start(s32[192]{0:T(256)} %param.15) | copy-start | bytes 2308
  17.1 52.2 %all-to-all-start = ((bf16[6,256,8,128]{3,2,0,1:T(8,128)(2,1)}), bf16[6,256,8,128]{3,2,0,1:T(8,128)(2,1)}, u32[]{:S(2)}, u32[]{:S(2)}) async-start(bf16[6,256,8,128]{3,2,0,1:T(8,128)(2,1)} %copy.95), calls=%async_computation | async-start | bytes 6291456 | tf_op jit(solution)/shard_map/all_to_all | solution.py:23
  28.7 564.1 %all-reduce.7.cloned.1.call-start = ((), (), s32[]{:S(2)}) async-start(), calls=%async_computation.4 | async-start | bytes 4194304 | tf_op jit(solution)/shard_map/psum | solution.py:165
  83.9 3.7 copy-start.4
  210.7 5.3 copy-start.6
  210.7 5.3 copy-start.10
  210.7 5.3 copy-start.14
  216.1 4.9 copy-start.5
  221.0 2.4 copy-start.13
  223.5 3.4 copy-start.12
  234.1 6.4 copy-start.2
  238.6 2.0 copy-start.3
  250.8 504.3 %all-reduce.9.cloned.1.call-start = ((), (), s32[]{:S(2)}) async-start(), calls=%async_computation.5 | async-start | bytes 4194304 | tf_op jit(solution)/shard_map/psum | solution.py:164
  596.9 153.9 %copy-start.7 = (f32[6,171]{1,0:T(8,128)S(1)}, f32[6,171]{1,0:T(8,128)}, u32[]{:S(2)}) copy-start(f32[6,171]{1,0:T(8,128)} %get-tuple-element.69) | copy-start | bytes 12316
  596.9 153.9 %copy-start.9 = (pred[6,171]{1,0:T(8,128)(4,1)S(1)}, pred[6,171]{1,0:T(8,128)(4,1)}, u32[]{:S(2)}) copy-start(pred[6,171]{1,0:T(8,128)(4,1)} %copy-done.8) | copy-start | bytes 3082
  600.1 150.7 %all-to-all-start.3 = ((bf16[192,8,4,128]{3,1,2,0:T(8,128)(2,1)}), bf16[192,8,4,128]{3,1,2,0:T(8,128)(2,1)S(1)}, u32[]{:S(2)}, u32[]{:S(2)}) async-start(bf16[192,8,4,128]{3,1,2,0:T(8,128)(2,1)} %copy.113), calls=%async_computation.3 | async-start | bytes 3145728 | tf_op jit(solution)/shard_map/all_to_all | solution.py:163
  750.8 10.3 %copy-start.1 = (bf16[6,171,4,128]{3,2,1,0:T(4,128)(2,1)S(1)}, bf16[6,171,4,128]{3,2,1,0:T(4,128)(2,1)}, u32[]{:S(2)}) copy-start(bf16[6,171,4,128]{3,2,1,0:T(4,128)(2,1)} %param.11) | copy-start | bytes 3151876
Sparse Core Ops, SparseCore 0:
  250.9 341.8 all-reduce.6
  595.5 89.6 all-reduce.8
